TPU v7x, 32 devices: a whole 2x2x4 slice. The times are simulated.
32 devices in a mesh: samp: 16 (over z, y, x), feat: 2 (over core).
Axes of the slice: x: 2, y: 2, z: 4, core: 2. Of those that a mesh axis runs over, the one named last changes fastest.
Arguments:
- design_matrix: bfloat16 [2048, 32768], P('samp', 'feat'), may hold values from -0.046875 to 0.046875
- labels: int32 [2048], P('samp'), may hold values from 0 to 1
- weights: float32 [16, 32768], P(None, ('feat', 'samp')), may hold values from -6 to 6
- lambdas: float32 [16], replicated, may hold values from 0.05 to 1
- sketch: bfloat16 [32768, 384], P(('feat', 'samp')), may hold values from -0.03125 to 0.03125
- sketch_values: float32 [384], replicated, may hold values from 0.05 to 2
Outputs:
- new_weights: float32 [16, 32768], P(None, ('feat', 'samp'))
All inputs are finite; a program needn't handle non-finite values.
Results may differ from a plain program's by a relative error of at most 0.004.
Values may be sent and summed in bfloat16 or wider, within the bound.
No kernel may reach another device: no remote copies, remote signals or barrier semaphores. Data moves between devices by JAX's collectives and lax.ppermute only.
A program may use at most 64 MiB of HBM per device.

v0:
```python
import jax
import jax.numpy as jnp
from jax import lax
from jax.sharding import PartitionSpec as P

ITERS = 2


def shards(design_matrix, labels, weights, lambdas, sketch, sketch_values):
    sketch_full = sketch.astype(jnp.float32)
    smallest = jnp.min(sketch_values)
    ratios = (smallest + lambdas[:, None]) / (sketch_values[None, :] + lambdas[:, None]) - 1.0

    def apply_rows(vector):
        vector_half = vector.astype(jnp.bfloat16)
        partial_rows = lax.dot_general(
            lax.all_gather(vector_half, "samp", axis=1, tiled=True),
            design_matrix,
            (((1,), (1,)), ((), ())),
            preferred_element_type=jnp.float32,
        )
        return lax.psum(partial_rows, "feat")

    def apply_columns(values):
        return lax.psum_scatter(
            lax.dot_general(
                design_matrix, values, (((0,), (1,)), ((), ())), preferred_element_type=jnp.float32
            ),
            "samp",
            scatter_dimension=0,
            tiled=True,
        ).T

    def precondition(residual):
        projected = jnp.dot(residual, sketch_full, precision=lax.Precision.HIGHEST)
        projected = lax.psum(projected, ("samp", "feat"))
        correction = lax.dot_general(
            ratios * projected,
            sketch_full,
            (((1,), (1,)), ((), ())),
            precision=lax.Precision.HIGHEST,
        )
        precond_res = residual + correction
        res_dot = lax.psum(jnp.sum(residual * precond_res, axis=1), ("samp", "feat"))
        return (precond_res, res_dot)

    logits = apply_rows(weights)
    probability = jax.nn.sigmoid(logits)
    hessian_diag = probability * (1.0 - probability)
    miss_rows = (probability - labels[None, :].astype(jnp.float32)).astype(jnp.bfloat16)
    gradient = apply_columns(miss_rows) + lambdas[:, None] * weights
    residual = -gradient
    precond_res, res_dot = precondition(residual)
    direction = precond_res
    update = jnp.zeros_like(residual)
    for iteration in range(ITERS):
        image_rows = apply_rows(direction)
        hess_dir = (
            apply_columns((hessian_diag * image_rows).astype(jnp.bfloat16))
            + lambdas[:, None] * direction
        )
        curvature = lax.psum(jnp.sum(direction * hess_dir, axis=1), ("samp", "feat"))
        step_size = res_dot / curvature
        update = update + step_size[:, None] * direction
        if iteration + 1 < ITERS:
            residual = residual - step_size[:, None] * hess_dir
            precond_res, new_dot = precondition(residual)
            direction = precond_res + (new_dot / res_dot)[:, None] * direction
            res_dot = new_dot
    return weights + update


def solution(mesh):
    return jax.shard_map(
        shards,
        mesh=mesh,
        in_specs=(
            P("samp", "feat"),
            P("samp"),
            P(None, ("feat", "samp")),
            P(),
            P(("feat", "samp"), None),
            P(),
        ),
        out_specs=P(None, ("feat", "samp")),
        check_vma=False,
    )
```

profile of v0, /device:TPU:10, one launch (start us, length us, event | category | flops | bytes accessed | tf_op | source)
XLA Modules:
  0.0 596.1 jit_solution(18189731865618623638)
XLA Ops:
  6.5 0.0 copy-start
  6.5 0.0 reduce-scatter.4.cloned.1.call-start
  6.5 0.7 convert_element_type.24
  7.3 0.8 convert_element_type.23
  8.1 33.0 %all_gather.9 = bf16[16,16384]{1,0:T(8,128)(2,1)S(1)} all-gather(bf16[16,1024]{1,0:T(8,128)(2,1)S(1)} %convert_element_type.23), channel_id=1, replica_groups=mesh['samp'=16,'feat'=2] {'samp'}, dimensions={1}, use_global_device_ids=true | all-gather | bytes 557056 | tf_op jit(solution)/shard_map/all_gather | solution.py:17
  41.1 3.4 fusion.22
  44.4 0.0 copy-start.3
  44.4 0.0 copy-start.2
  44.4 0.0 copy-start.1
  44.5 2.6 psum.63
  47.1 3.8 convolution_bitcast_fusion.2
  51.0 0.0 reduce-scatter.4.cloned.1.call-update
  51.0 0.0 reduce-scatter.6.cloned.1.call-start
  51.0 0.0 copy-done.3
  51.0 0.6 reduce_min.9
  51.6 0.0 copy-done.2
  51.6 0.6 broadcast_add_fusion
  52.3 73.3 %reduce-scatter.4.cloned.1.call-done = f32[1024,16]{0,1:T(8,128)} async-done(((f32[16384,16]{0,1:T(8,128)}), f32[1024,16]{0,1:T(8,128)}) %reduce-scatter.4.cloned.1.call-update) | async-done | bytes 65552 | tf_op jit(solution)/shard_map/reduce_scatter | solution.py:25
  125.6 0.0 copy-done.1
  125.6 0.9 fusion.2
  126.6 0.0 copy-done
  126.6 0.4 fusion.23
  127.0 50.1 %psum.64 = f32[16,384]{1,0:T(8,128)S(1)} all-reduce(f32[16,384]{1,0:T(8,128)S(1)} %fusion.23), channel_id=1, replica_groups=mesh['samp'=16,'feat'=2] {'samp','feat'}, use_global_device_ids=true, to_apply=%region_3.0 | all-reduce | flops 6144 | bytes 49152 | tf_op jit(solution)/shard_map/psum | solution.py:36
  177.1 0.7 fusion.21
  177.8 32.0 %all_gather.10 = bf16[16,16384]{1,0:T(8,128)(2,1)S(1)} all-gather(bf16[16,1024]{1,0:T(8,128)(2,1)S(1)} %get-tuple-element.9), channel_id=1, replica_groups=mesh['samp'=16,'feat'=2] {'samp'}, dimensions={1}, use_global_device_ids=true | all-gather | bytes 557056 | tf_op jit(solution)/shard_map/all_gather | solution.py:17
  209.8 3.4 fusion.24
  213.1 2.5 psum.66
  215.6 3.8 convolution_bitcast_fusion.1
  219.5 0.0 reduce-scatter.6.cloned.1.call-update
  219.5 0.0 reduce-scatter.8.cloned.1.call-start
  219.5 71.6 %reduce-scatter.6.cloned.1.call-done = f32[1024,16]{0,1:T(8,128)} async-done(((f32[16384,16]{0,1:T(8,128)}), f32[1024,16]{0,1:T(8,128)}) %reduce-scatter.6.cloned.1.call-update) | async-done | bytes 65552 | tf_op jit(solution)/shard_map/reduce_scatter | solution.py:25
  291.1 1.0 multiply_reduce_fusion.1
  292.1 49.7 %all-reduce = (f32[16]{0:T(128)S(1)}, f32[16]{0:T(128)S(1)}) all-reduce(f32[16]{0:T(128)S(1)} %get-tuple-element.6, f32[16]{0:T(128)S(1)} %get-tuple-element.5), channel_id=1, replica_groups=mesh['samp'=16,'feat'=2] {'samp','feat'}, use_global_device_ids=true, to_apply=%region_5.0 | all-reduce | flops 32 | bytes 256 | tf_op jit(solution)/shard_map/psum | solution.py:44
  341.9 0.9 multiply_subtract_fusion
  342.8 0.4 fusion.25
  343.2 38.3 %psum.68 = f32[16,384]{1,0:T(8,128)S(1)} all-reduce(f32[16,384]{1,0:T(8,128)S(1)} %fusion.25), channel_id=1, replica_groups=mesh['samp'=16,'feat'=2] {'samp','feat'}, use_global_device_ids=true, to_apply=%region_10.0 | all-reduce | flops 6144 | bytes 49152 | tf_op jit(solution)/shard_map/psum | solution.py:36
  381.5 0.8 multiply_reduce_fusion
  382.3 41.9 %psum.69 = f32[16]{0:T(128)S(1)} all-reduce(f32[16]{0:T(128)S(1)} %get-tuple-element.11), channel_id=1, replica_groups=mesh['samp'=16,'feat'=2] {'samp','feat'}, use_global_device_ids=true, to_apply=%region_12.0 | all-reduce | flops 16 | bytes 128 | tf_op jit(solution)/shard_map/psum | solution.py:44
  424.2 0.1 fusion.20
  424.3 31.8 %all_gather.11 = bf16[16,16384]{1,0:T(8,128)(2,1)S(1)} all-gather(bf16[16,1024]{1,0:T(8,128)(2,1)S(1)} %fusion.20), channel_id=1, replica_groups=mesh['samp'=16,'feat'=2] {'samp'}, dimensions={1}, use_global_device_ids=true | all-gather | bytes 557056 | tf_op jit(solution)/shard_map/all_gather | solution.py:17
  456.1 3.4 fusion.26
  459.5 2.5 psum.70
  462.0 3.9 convolution_bitcast_fusion
  465.8 0.0 reduce-scatter.8.cloned.1.call-update
  465.8 72.2 %reduce-scatter.8.cloned.1.call-done = f32[1024,16]{0,1:T(8,128)} async-done(((f32[16384,16]{0,1:T(8,128)}), f32[1024,16]{0,1:T(8,128)}) %reduce-scatter.8.cloned.1.call-update) | async-done | bytes 65552 | tf_op jit(solution)/shard_map/reduce_scatter | solution.py:25
  538.1 1.0 fusion.1
  539.1 49.8 %psum.71 = f32[16]{0:T(128)S(1)} all-reduce(f32[16]{0:T(128)S(1)} %fusion.1), channel_id=1, replica_groups=mesh['samp'=16,'feat'=2] {'samp','feat'}, use_global_device_ids=true, to_apply=%region_16.0 | all-reduce | flops 16 | bytes 128 | tf_op jit(solution)/shard_map/psum | solution.py:62
  588.9 0.7 add_add_fusion
  (3 shorter events, 0.0 us)
Async XLA Ops:
  6.5 120.0 %copy-start = (bf16[1024,384]{1,0:T(8,128)(2,1)S(1)}, bf16[1024,384]{1,0:T(8,128)(2,1)}, u32[]{:S(2)}) copy-start(bf16[1024,384]{1,0:T(8,128)(2,1)} %param.10) | copy-start | bytes 2359300
  6.5 119.1 %reduce-scatter.4.cloned.1.call-start = ((), (), s32[]{:S(2)}) async-start(), calls=%async_computation.3 | async-start | bytes 1114112 | tf_op jit(solution)/shard_map/reduce_scatter | solution.py:25
  44.4 6.6 %copy-start.3 = (f32[384]{0:T(512)S(1)}, f32[384]{0:T(512)}, u32[]{:S(2)}) copy-start(f32[384]{0:T(512)} %param.11) | copy-start | bytes 4612
  44.4 7.2 %copy-start.2 = (f32[16]{0:T(128)S(1)}, f32[16]{0:T(128)}, u32[]{:S(2)}) copy-start(f32[16]{0:T(128)} %param.9) | copy-start | bytes 196
  44.4 81.2 %copy-start.1 = (f32[16,1024]{1,0:T(8,128)S(1)}, f32[16,1024]{1,0:T(8,128)}, u32[]{:S(2)}) copy-start(f32[16,1024]{1,0:T(8,128)} %param.8) | copy-start | bytes 196612
  51.0 240.1 %reduce-scatter.6.cloned.1.call-start = ((), (), s32[]{:S(2)}) async-start(), calls=%async_computation.4 | async-start | bytes 1114112 | tf_op jit(solution)/shard_map/reduce_scatter | solution.py:25
  219.5 318.6 %reduce-scatter.8.cloned.1.call-start = ((), (), s32[]{:S(2)}) async-start(), calls=%async_computation.5 | async-start | bytes 1114112 | tf_op jit(solution)/shard_map/reduce_scatter | solution.py:25
Sparse Core Ops, SparseCore 0:
  51.1 74.4 reduce-scatter.3
  219.6 71.4 reduce-scatter.5
  466.0 72.0 reduce-scatter.7
where the time goes:
time: 597 us; the launch traced here: 596 us
  blocking collectives  334 us (56%)
  waiting for transfers between devices  217 us (36%)
  matrix products  24.1 us (4%)
  between operations  13.2 us (2%)
  other arithmetic  7.54 us (1%)
    reduce_scatter x3, waiting for transfers between devices, apply_columns(): lax.psum_scatter(lax.dot_general(design_matrix, values, (((0,), (1,)), ((...  217 us
    all_gather x3, blocking collectives, apply_rows(): lax.all_gather(vector_half, 'samp', axis=1, tiled=True)  96.7 us
    psum x2, blocking collectives, precondition(): lax.psum(jnp.sum(residual * precond_res, axis=1), ('samp', 'feat'))  91.6 us
    psum x2, blocking collectives, precondition(): projected = lax.psum(projected, ('samp', 'feat'))  88.3 us
    psum x1, blocking collectives, shards(): lax.psum(jnp.sum(direction * hess_dir, axis=1), ('samp', 'feat'))  49.8 us
  transfers between devices with their start and end apart: 3, of which 3 were waited for; matrix products, arithmetic and copies ran while one was open for 0% of the time, Pallas kernels for 0%

commit v1 on v0

--- a/solution.py
+++ b/solution.py
@@ -41,7 +41,7 @@
             precision=lax.Precision.HIGHEST,
         )
         precond_res = residual + correction
-        res_dot = lax.psum(jnp.sum(residual * precond_res, axis=1), ("samp", "feat"))
+        res_dot = lax.psum(lax.psum(jnp.sum(residual * precond_res, axis=1), "feat"), "samp")
         return (precond_res, res_dot)
 
     logits = apply_rows(weights)

time: 597 us -> 637 us (1.067)
  blocking collectives: 334 us -> 374 us
    psum x1 -> x2, blocking collectives: 49.8 us -> 99.4 us  [shards(): lax.psum(jnp.sum(direction * hess_dir, axis=1), ('samp', 'feat'))]
    psum x2 -> x4, blocking collectives: 91.6 us -> 63.1 us  [the longest x2 58.2 us: precondition(): lax.psum(lax.psum(jnp.sum(residual * precond_res, axis=1), 'feat'), 'samp')]
    psum x2, blocking collectives: 88.3 us -> 98 us  [precondition(): projected = lax.psum(projected, ('samp', 'feat'))]
    all_gather x3, blocking collectives: 96.7 us -> 106 us  [apply_rows(): lax.all_gather(vector_half, 'samp', axis=1, tiled=True)]
where the time goes in v1:
time: 637 us; the launch traced here: 636 us
  blocking collectives  374 us (59%)
  waiting for transfers between devices  216 us (34%)
  matrix products  24.1 us (4%)
  between operations  13.2 us (2%)
  other arithmetic  7.54 us (1%)
    reduce_scatter x3, waiting for transfers between devices, apply_columns(): lax.psum_scatter(lax.dot_general(design_matrix, values, (((0,), (1,)), ((...  216 us
    all_gather x3, blocking collectives, apply_rows(): lax.all_gather(vector_half, 'samp', axis=1, tiled=True)  106 us
    psum x2, blocking collectives, shards(): lax.psum(jnp.sum(direction * hess_dir, axis=1), ('samp', 'feat'))  99.4 us
    psum x2, blocking collectives, precondition(): projected = lax.psum(projected, ('samp', 'feat'))  98 us
    psum x2, blocking collectives, precondition(): lax.psum(lax.psum(jnp.sum(residual * precond_res, axis=1), 'feat'), 'samp')  58.2 us
  transfers between devices with their start and end apart: 3, of which 3 were waited for; matrix products, arithmetic and copies ran while one was open for 0% of the time, Pallas kernels for 0%

profile of v1, /device:TPU:10, one launch (start us, length us, event | category | flops | bytes accessed | tf_op | source)
XLA Modules:
  0.0 635.8 jit_solution(2719334111356953145)
XLA Ops:
  6.5 0.0 copy-start
  6.5 0.0 reduce-scatter.4.cloned.1.call-start
  6.5 0.7 convert_element_type.24
  7.3 0.8 convert_element_type.23
  8.1 33.0 %all_gather.9 = bf16[16,16384]{1,0:T(8,128)(2,1)S(1)} all-gather(bf16[16,1024]{1,0:T(8,128)(2,1)S(1)} %convert_element_type.23), channel_id=1, replica_groups=mesh['samp'=16,'feat'=2] {'samp'}, dimensions={1}, use_global_device_ids=true | all-gather | bytes 557056 | tf_op jit(solution)/shard_map/all_gather | solution.py:17
  41.1 3.4 fusion.22
  44.4 0.0 copy-start.3
  44.4 0.0 copy-start.2
  44.4 0.0 copy-start.1
  44.5 2.6 psum.77
  47.1 3.8 convolution_bitcast_fusion.2
  51.0 0.0 reduce-scatter.4.cloned.1.call-update
  51.0 0.0 reduce-scatter.6.cloned.1.call-start
  51.0 0.0 copy-done.3
  51.0 0.6 reduce_min.9
  51.6 0.0 copy-done.2
  51.6 0.6 broadcast_add_fusion
  52.3 73.3 %reduce-scatter.4.cloned.1.call-done = f32[1024,16]{0,1:T(8,128)} async-done(((f32[16384,16]{0,1:T(8,128)}), f32[1024,16]{0,1:T(8,128)}) %reduce-scatter.4.cloned.1.call-update) | async-done | bytes 65552 | tf_op jit(solution)/shard_map/reduce_scatter | solution.py:25
  125.6 0.0 copy-done.1
  125.6 0.9 fusion.2
  126.6 0.0 copy-done
  126.6 0.4 fusion.23
  127.0 50.1 %psum.78 = f32[16,384]{1,0:T(8,128)S(1)} all-reduce(f32[16,384]{1,0:T(8,128)S(1)} %fusion.23), channel_id=1, replica_groups=mesh['samp'=16,'feat'=2] {'samp','feat'}, use_global_device_ids=true, to_apply=%region_3.0 | all-reduce | flops 6144 | bytes 49152 | tf_op jit(solution)/shard_map/psum | solution.py:36
  177.1 0.7 fusion.21
  177.8 32.0 %all_gather.10 = bf16[16,16384]{1,0:T(8,128)(2,1)S(1)} all-gather(bf16[16,1024]{1,0:T(8,128)(2,1)S(1)} %get-tuple-element.7), channel_id=1, replica_groups=mesh['samp'=16,'feat'=2] {'samp'}, dimensions={1}, use_global_device_ids=true | all-gather | bytes 557056 | tf_op jit(solution)/shard_map/all_gather | solution.py:17
  209.8 3.4 fusion.24
  213.1 2.5 psum.81
  215.6 3.8 convolution_bitcast_fusion.1
  219.5 0.0 reduce-scatter.6.cloned.1.call-update
  219.5 0.0 reduce-scatter.8.cloned.1.call-start
  219.5 71.6 %reduce-scatter.6.cloned.1.call-done = f32[1024,16]{0,1:T(8,128)} async-done(((f32[16384,16]{0,1:T(8,128)}), f32[1024,16]{0,1:T(8,128)}) %reduce-scatter.6.cloned.1.call-update) | async-done | bytes 65552 | tf_op jit(solution)/shard_map/reduce_scatter | solution.py:25
  291.1 1.0 multiply_reduce_fusion.1
  292.1 49.7 %psum.82 = f32[16]{0:T(128)S(1)} all-reduce(f32[16]{0:T(128)S(1)} %get-tuple-element.5), channel_id=1, replica_groups=mesh['samp'=16,'feat'=2] {'samp','feat'}, use_global_device_ids=true, to_apply=%region_10.0 | all-reduce | flops 16 | bytes 128 | tf_op jit(solution)/shard_map/psum | solution.py:62
  341.8 2.4 psum.79
  344.3 29.1 %psum.80 = f32[16]{0:T(128)S(1)} all-reduce(f32[16]{0:T(128)S(1)} %psum.79), channel_id=1, replica_groups=mesh['samp'=16,'feat'=2] {'samp'}, use_global_device_ids=true, to_apply=%region_6.0 | all-reduce | flops 16 | bytes 128 | tf_op jit(solution)/shard_map/psum | solution.py:44
  373.4 0.9 multiply_subtract_fusion
  374.3 0.4 fusion.25
  374.8 47.9 %psum.83 = f32[16,384]{1,0:T(8,128)S(1)} all-reduce(f32[16,384]{1,0:T(8,128)S(1)} %fusion.25), channel_id=1, replica_groups=mesh['samp'=16,'feat'=2] {'samp','feat'}, use_global_device_ids=true, to_apply=%region_11.0 | all-reduce | flops 6144 | bytes 49152 | tf_op jit(solution)/shard_map/psum | solution.py:36
  422.7 0.8 multiply_reduce_fusion
  423.5 2.5 psum.84
  426.0 29.1 %psum.85 = f32[16]{0:T(128)S(1)} all-reduce(f32[16]{0:T(128)S(1)} %psum.84), channel_id=1, replica_groups=mesh['samp'=16,'feat'=2] {'samp'}, use_global_device_ids=true, to_apply=%region_14.0 | all-reduce | flops 16 | bytes 128 | tf_op jit(solution)/shard_map/psum | solution.py:44
  455.1 0.1 fusion.20
  455.2 41.4 %all_gather.11 = bf16[16,16384]{1,0:T(8,128)(2,1)S(1)} all-gather(bf16[16,1024]{1,0:T(8,128)(2,1)S(1)} %fusion.20), channel_id=1, replica_groups=mesh['samp'=16,'feat'=2] {'samp'}, dimensions={1}, use_global_device_ids=true | all-gather | bytes 557056 | tf_op jit(solution)/shard_map/all_gather | solution.py:17
  496.6 3.4 fusion.26
  500.0 2.5 psum.86
  502.5 3.9 convolution_bitcast_fusion
  506.3 0.0 reduce-scatter.8.cloned.1.call-update
  506.3 71.5 %reduce-scatter.8.cloned.1.call-done = f32[1024,16]{0,1:T(8,128)} async-done(((f32[16384,16]{0,1:T(8,128)}), f32[1024,16]{0,1:T(8,128)}) %reduce-scatter.8.cloned.1.call-update) | async-done | bytes 65552 | tf_op jit(solution)/shard_map/reduce_scatter | solution.py:25
  577.8 1.0 fusion.1
  578.9 49.7 %psum.87 = f32[16]{0:T(128)S(1)} all-reduce(f32[16]{0:T(128)S(1)} %fusion.1), channel_id=1, replica_groups=mesh['samp'=16,'feat'=2] {'samp','feat'}, use_global_device_ids=true, to_apply=%region_18.0 | all-reduce | flops 16 | bytes 128 | tf_op jit(solution)/shard_map/psum | solution.py:62
  628.6 0.7 add_add_fusion
  (3 shorter events, 0.0 us)
Async XLA Ops:
  6.5 120.0 %copy-start = (bf16[1024,384]{1,0:T(8,128)(2,1)S(1)}, bf16[1024,384]{1,0:T(8,128)(2,1)}, u32[]{:S(2)}) copy-start(bf16[1024,384]{1,0:T(8,128)(2,1)} %param.10) | copy-start | bytes 2359300
  6.5 119.1 %reduce-scatter.4.cloned.1.call-start = ((), (), s32[]{:S(2)}) async-start(), calls=%async_computation.3 | async-start | bytes 1114112 | tf_op jit(solution)/shard_map/reduce_scatter | solution.py:25
  44.4 6.6 %copy-start.3 = (f32[384]{0:T(512)S(1)}, f32[384]{0:T(512)}, u32[]{:S(2)}) copy-start(f32[384]{0:T(512)} %param.11) | copy-start | bytes 4612
  44.4 7.2 %copy-start.2 = (f32[16]{0:T(128)S(1)}, f32[16]{0:T(128)}, u32[]{:S(2)}) copy-start(f32[16]{0:T(128)} %param.9) | copy-start | bytes 196
  44.4 81.2 %copy-start.1 = (f32[16,1024]{1,0:T(8,128)S(1)}, f32[16,1024]{1,0:T(8,128)}, u32[]{:S(2)}) copy-start(f32[16,1024]{1,0:T(8,128)} %param.8) | copy-start | bytes 196612
  51.0 240.1 %reduce-scatter.6.cloned.1.call-start = ((), (), s32[]{:S(2)}) async-start(), calls=%async_computation.4 | async-start | bytes 1114112 | tf_op jit(solution)/shard_map/reduce_scatter | solution.py:25
  219.5 358.3 %reduce-scatter.8.cloned.1.call-start = ((), (), s32[]{:S(2)}) async-start(), calls=%async_computation.5 | async-start | bytes 1114112 | tf_op jit(solution)/shard_map/reduce_scatter | solution.py:25
Sparse Core Ops, SparseCore 0:
  51.1 74.4 reduce-scatter.3
  219.6 71.4 reduce-scatter.5
  506.4 71.3 reduce-scatter.7
